TPU v7x, 256 devices: a whole 4x4x8 slice. The times are simulated.
256 devices in a mesh: gx: 2 (over x_lo), gy: 8 (over x_hi, y), gz: 16 (over z, core).
Axes of the slice: x: 4 (x_hi: 2, x_lo: 2; x = x_hi * 2 + x_lo), y: 4, z: 8, core: 2. Of those that a mesh axis runs over, the one named last changes fastest.
Arguments:
- volume: bfloat16 [32, 64, 64, 256], P(None, 'gx', 'gy', 'gz'), may hold values from -6 to 6
- weight_a: bfloat16 [3, 3, 3, 32, 64], replicated, may hold values from -0.21875 to 0.21875
- bias_a: float32 [64], replicated, may hold values from -3 to 3
- weight_b: bfloat16 [3, 3, 3, 64, 128], replicated, may hold values from -0.15625 to 0.15625
- bias_b: float32 [128], replicated, may hold values from -3 to 3
- cotangent: bfloat16 [128, 32, 32, 128], P(None, ('gx', 'gz'), 'gy'), may hold values from -24 to 24
Outputs:
- features: bfloat16 [128, 32, 32, 128], P(None, ('gx', 'gz'), 'gy')
- grad_input: bfloat16 [32, 64, 64, 256], P(None, 'gx', 'gy', 'gz')
- grad_weight_a: float32 [3, 3, 3, 32, 64], replicated
- grad_bias_a: float32 [64], replicated
- grad_weight_b: float32 [3, 3, 3, 64, 128], replicated
- grad_bias_b: float32 [128], replicated
All inputs are finite; a program needn't handle non-finite values.
Results may differ from a plain program's by a relative error of at most 0.012.
Values may be sent and summed in bfloat16 or wider, within the bound.
A program may use at most 128 MiB of HBM per device.

v0:
```python
import math

import jax
import jax.numpy as jnp
from jax import lax
from jax.sharding import Mesh
from jax.sharding import PartitionSpec as P

GX_GY_GZ = ("gx", "gy", "gz_0", "gz_1")
GZ = ("gz_0", "gz_1")
GX_GZ = ("gx", "gz_0", "gz_1")


def padded_2(block, sides, width):
    for axis, dim in sides:
        count = lax.axis_size(axis)
        forward = [(i, i + 1) for i in range(count - 1)]
        backward = [(target, source) for source, target in forward]
        low = lax.ppermute(
            lax.slice_in_dim(block, block.shape[dim] - width, None, axis=dim), axis, forward
        )
        high = lax.ppermute(lax.slice_in_dim(block, 0, width, axis=dim), axis, backward)
        block = jnp.concatenate([low, block, high], axis=dim)
    return block


def cut_along(array, dim, length):
    lengths = array.shape
    pieces = array.reshape(*lengths[:dim], length, lengths[dim] // length, *lengths[dim + 1 :])
    return jnp.moveaxis(pieces, dim, 0)


def laid_out(pieces, dim):
    lengths = list(pieces.shape[1:])
    lengths[dim] *= pieces.shape[0]
    return jnp.moveaxis(pieces, 0, dim).reshape(lengths)


def moved_by_axis(pieces, axes, order):
    inside = pieces.shape[1:]
    result = pieces.reshape(*(lax.axis_size(a) for a in axes), *inside)
    for k in order:
        result = lax.all_to_all(result, axes[k], k, k, tiled=True)
    return result.reshape(-1, *inside)


def exchange_by_axis(array, axes, order, split_dim, concat_dim):
    pieces = cut_along(array, split_dim, lax.axis_size(axes))
    return laid_out(moved_by_axis(pieces, axes, order), concat_dim)


def together(arrays, axis):
    ends = [0]
    for a in arrays:
        ends.append(ends[-1] + a.size)
    total = lax.psum(jnp.concatenate([a.ravel() for a in arrays]), axis)
    return tuple((total[b:e].reshape(a.shape) for a, b, e in zip(arrays, ends, ends[1:])))


def activate(value):
    return value * jax.nn.sigmoid(value)


def slope_of(value):
    sigma = jax.nn.sigmoid(value)
    return sigma + value * sigma * (1.0 - sigma)


def conv_valid(padded, weight):
    result = lax.conv_general_dilated(
        padded[None],
        weight,
        (1, 1, 1),
        "VALID",
        dimension_numbers=("NCDHW", "DHWIO", "NCDHW"),
        preferred_element_type=jnp.float32,
    )
    return result[0]


def flipped(weight):
    return jnp.transpose(weight[::-1, ::-1, ::-1], (0, 1, 2, 4, 3))


def average_pool(field):
    shape = field.shape
    split = field.reshape(shape[0], shape[1] // 2, 2, shape[2] // 2, 2, shape[3] // 2, 2)
    return jnp.sum(split, axis=(2, 4, 6)) * 0.125


def spread_back(field):
    shape = field.shape
    larger = jnp.broadcast_to(
        field[:, :, None, :, None, :, None], (shape[0], shape[1], 2, shape[2], 2, shape[3], 2)
    )
    return larger.reshape(shape[0], 2 * shape[1], 2 * shape[2], 2 * shape[3])


def weight_terms(padded, grad):
    result = lax.conv_general_dilated(
        padded[None],
        grad[None],
        (1, 1, 1),
        "VALID",
        dimension_numbers=("CNDHW", "IODHW", "NCDHW"),
        preferred_element_type=jnp.float32,
    )
    return jnp.transpose(result, (2, 3, 4, 0, 1))


def fine_halo(field):
    return padded_2(field, (("gx", 1), ("gy", 2), (GZ, 3)), 1)


def coarse_halo(field):
    return padded_2(field, (("gx", 1), ("gy", 2), (GZ, 3)), 1)


def on_device(volume, weight_a, bias_a, weight_b, bias_b, cotangent):
    devices_all = lax.axis_size("gx") * lax.axis_size("gy") * lax.axis_size(GZ)
    cells_fine = volume.shape[1] * volume.shape[2] * volume.shape[3] * devices_all
    scale_a = 1.0 / math.sqrt(cells_fine)
    scale_b = 1.0 / math.sqrt(cells_fine // 8)
    padded_a = fine_halo(volume)
    before_a = conv_valid(padded_a, weight_a) + bias_a[:, None, None, None]
    pooled = average_pool(activate(before_a)).astype(jnp.bfloat16)
    padded_b = coarse_halo(pooled)
    before_b = conv_valid(padded_b, weight_b) + bias_b[:, None, None, None]
    features_block = activate(before_b).astype(jnp.bfloat16)
    features = exchange_by_axis(features_block, GZ, (1, 0), 1, 3)
    cotangent_block = lax.all_to_all(cotangent, GZ, split_axis=3, concat_axis=1, tiled=True)
    grad_b = (cotangent_block * slope_of(before_b)).astype(jnp.bfloat16)
    grad_pooled = conv_valid(coarse_halo(grad_b), flipped(weight_b)).astype(jnp.bfloat16)
    partial_wb = weight_terms(padded_b, grad_b)
    partial_bb = jnp.sum(grad_b, axis=(1, 2, 3), dtype=jnp.float32)
    grad_a = (spread_back(grad_pooled) * 0.125 * slope_of(before_a)).astype(jnp.bfloat16)
    partial_wa = weight_terms(padded_a, grad_a)
    partial_ba = jnp.sum(grad_a, axis=(1, 2, 3), dtype=jnp.float32)
    grad_input = conv_valid(fine_halo(grad_a), flipped(weight_a)).astype(jnp.bfloat16)
    summed_wa, summed_ba, summed_wb, summed_bb = together(
        (partial_wa, partial_ba, partial_wb, partial_bb), GX_GY_GZ
    )
    return (
        features,
        grad_input,
        summed_wa * scale_a,
        summed_ba * scale_a,
        summed_wb * scale_b,
        summed_bb * scale_b,
    )


def solution(mesh):
    finer = Mesh(
        mesh.devices.reshape(mesh.shape["gx"], mesh.shape["gy"], 8, 2), ("gx", "gy", "gz_0", "gz_1")
    )
    return jax.shard_map(
        on_device,
        mesh=finer,
        in_specs=(P(None, "gx", "gy", GZ), P(), P(), P(), P(), P(None, GX_GZ, "gy", None)),
        out_specs=(P(None, GX_GZ, "gy", None), P(None, "gx", "gy", GZ), P(), P(), P(), P()),
        check_vma=False,
    )
```

profile of v0, /device:TPU:1, one launch (start us, length us, event | category | flops | bytes accessed | tf_op | source)
XLA Modules:
  0.0 505.8 jit_solution(1847951043806130101)
XLA Ops:
  7.2 3.2 fusion.46
  12.7 3.9 collective-permute-start
  25.7 3.2 collective-permute-start.2
  30.8 3.8 collective-permute-done.3
  34.7 7.0 %collective-permute-start.4 = (bf16[32,34,10,1]{1,0,3,2:T(8,128)(2,1)S(1)}, bf16[32,34,10,1]{1,0,3,2:T(8,128)(2,1)S(1)}, u32[]{:S(2)}, u32[]{:S(2)}) collective-permute-start(bf16[32,34,10,1]{1,0,3,2:T(8,128)(2,1)S(1)} %get-tuple-element.40), channel_id=1, source_target_pairs={{0,1},{1,2},{2,3},{3,4},{4,5},{5,6},{6,7},{7,8},{8,9},{9,10},{10,1... | collective-permute-start | bytes 65288 | tf_op jit(solution)/shard_map/ppermute | solution.py:19
  44.0 3.5 collective-permute-done.5
  50.2 4.9 copy.132
  56.8 8.4 %multiply_add_fusion = (f32[32,8,8,3,64]{4,2,3,1,0:T(8,128)}, f32[32,8,8,3,64]{4,2,3,1,0:T(8,128)S(1)}) fusion(f32[64]{0:T(128)S(1)} %copy-done.23, bf16[3,3,3,32,64]{4,3,2,1,0:T(8,128)(2,1)S(1)} %copy-done.25, bf16[32,34,10,1,7,2]{0,4,5,2,1,3:T(8,128)(2,1)S(1)} %slice.117, bf16[32,34,10,1,8,3]{0,4,5,2,1,3:T(8,128)(2,1)} %copy.132, ...), kind=kOutput, calls=%fused_computation.17 | convolution fusion | flops 685627392 | bytes 4083480 | tf_op jit(solution)/shard_map/conv_general_dilated | solution.py:70
  70.2 3.1 collective-permute-done.7
  73.3 3.2 collective-permute-start.8
  77.8 3.4 collective-permute-done.9
  81.3 4.7 collective-permute-start.10
  88.7 11.8 %all-to-all-start.2 = ((bf16[128,1,4,128]{0,2,1,3:T(4,128)(2,1)}), bf16[128,1,4,128]{0,2,1,3:T(4,128)(2,1)S(1)}, u32[]{:S(2)}, u32[]{:S(2)}) async-start(bf16[128,1,4,128]{0,2,1,3:T(4,128)(2,1)} %copy.141), calls=%async_computation.2 | async-start | bytes 262144 | tf_op jit(solution)/shard_map/all_to_all | solution.py:131
  103.6 5.7 %all-to-all-done.2 = bf16[128,1,4,128]{0,2,1,3:T(4,128)(2,1)S(1)} async-done(((bf16[128,1,4,128]{0,2,1,3:T(4,128)(2,1)}), bf16[128,1,4,128]{0,2,1,3:T(4,128)(2,1)S(1)}, u32[]{:S(2)}, u32[]{:S(2)}) %all-to-all-start.2) | async-done | bytes 131104 | tf_op jit(solution)/shard_map/all_to_all | solution.py:131
  112.6 3.4 fusion.54
  116.0 7.7 %copy.151 = bf16[1,32,34,10,18]{1,0,4,3,2:T(2,128)(2,1)} copy(bf16[1,32,34,10,18]{2,1,4,3,0:T(8,128)(2,1)} %fusion.54) | data formatting | bytes 783360 | tf_op jit(solution)/shard_map/broadcast_in_dim | solution.py:71
  123.7 4.2 copy.150
  127.9 6.6 %collective-permute-start.14 = (bf16[128,18,1,8]{0,3,2,1:T(8,128)(2,1)S(1)}, bf16[128,18,1,8]{0,3,2,1:T(8,128)(2,1)S(1)}, u32[]{:S(2)}, u32[]{:S(2)}) collective-permute-start(bf16[128,18,1,8]{0,3,2,1:T(8,128)(2,1)S(1)} %get-tuple-element.56), channel_id=1, source_target_pairs={{0,16},{16,32},{32,48},{48,64},{64,80},{80,96},{96,112},{1,17},{17... | collective-permute-start | bytes 110600 | tf_op jit(solution)/shard_map/ppermute | solution.py:19
  135.9 3.9 all_to_all.19
  140.5 4.0 all-to-all-start.1
  144.6 3.7 collective-permute-start.16
  150.4 3.8 collective-permute-done.17
  159.0 4.3 collective-permute-start.18
  164.6 4.2 fusion.30
  169.2 4.3 collective-permute-start.20
  178.3 5.7 %collective-permute-done.21 = bf16[64,34,1,16]{0,2,3,1:T(2,128)(2,1)S(1)} collective-permute-done((bf16[64,34,1,16]{0,2,3,1:T(2,128)(2,1)S(1)}, bf16[64,34,1,16]{0,2,3,1:T(2,128)(2,1)S(1)}, u32[]{:S(2)}, u32[]{:S(2)}) %collective-permute-start.21) | collective-permute-done | bytes 69664 | tf_op jit(solution)/shard_map/ppermute | solution.py:22
  184.9 4.8 collective-permute-start.22
  191.9 24.5 %fusion.18 = f32[3,3,3,32,64]{4,3,2,1,0:T(8,128)} fusion(bf16[1,32,34,10,18]{1,0,4,3,2:T(2,128)(2,1)S(1)} %copy-done.8, bf16[1,64,32,8,16]{1,3,4,2,0:T(8,128)(2,1)S(1)} %get-tuple-element.39), kind=kOutput, calls=%fused_computation.27 | convolution fusion | flops 452984832 | bytes 1137152 | tf_op jit(solution)/shard_map/transpose | solution.py:108
  217.7 8.6 %concatenate.51 = f32[276672]{0:T(1024)} concatenate(f32[55296]{0:T(1024)S(1)} %reshape.130, f32[64]{0:T(128)S(1)} %copy-done.24, f32[221184]{0:T(1024)S(1)} %bitcast.99, f32[128]{0:T(128)S(1)} %copy-done.22), dimensions={0} | concatenate | bytes 2213376 | tf_op jit(solution)/shard_map/concatenate | solution.py:56
  228.1 4.1 maximum_bitcast_fusion
  234.1 11.4 %select_convert_fusion = bf16[32,8,8,3,32]{4,2,3,1,0:T(8,128)(2,1)S(1)} fusion(pred[8,3]{0,1:T(4,128)(4,1)S(1)} %copy-done.28, bf16[3,3,3,32,64]{4,3,2,1,0:T(8,128)(2,1)S(1)} %copy-done.26, bf16[64,34,10,1,7,2]{0,4,5,2,1,3:T(8,128)(2,1)S(1)} %slice.125, bf16[64,34,10,1,8,3]{0,4,5,2,1,3:T(8,128)(2,1)S(1)} %copy.148), kind=kOutput, calls=%fused_computation.16 | convolution fusion | flops 685092864 | bytes 2157592 | tf_op jit(solution)/shard_map/conv_general_dilated | solution.py:70
  248.8 243.3 %all-reduce.2.cloned.1.call-done = f32[276672]{0:T(1024)} async-done(((f32[276672]{0:T(1024)}), f32[276672]{0:T(1024)}) %all-reduce.2.cloned.1.call-update) | async-done | bytes 1106704 | tf_op jit(solution)/shard_map/psum | solution.py:56
  (144 shorter events, 68.6 us)
Async XLA Ops:
  7.2 94.4 %copy-start = (bf16[3,3,3,64,128]{4,3,2,1,0:T(8,128)(2,1)S(1)}, bf16[3,3,3,64,128]{4,3,2,1,0:T(8,128)(2,1)}, u32[]{:S(2)}) copy-start(bf16[3,3,3,64,128]{4,3,2,1,0:T(8,128)(2,1)} %param.9) | copy-start | bytes 1327108
  12.7 7.2 %collective-permute-start = (bf16[32,1,8,16]{0,3,2,1:T(8,128)(2,1)S(1)}, bf16[32,1,8,16]{0,3,2,1:T(8,128)(2,1)S(1)}, u32[]{:S(2)}, u32[]{:S(2)}) collective-permute-start(bf16[32,1,8,16]{0,3,2,1:T(8,128)(2,1)S(1)} %copy.164), channel_id=1, source_target_pairs={{0,128},{1,129},{2,130},{3,131},{4,132},{5,133},{6,134},{7,135},{8... | collective-permute-start | bytes 24584 | tf_op jit(solution)/shard_map/ppermute | solution.py:19
  17.9 4.7 collective-permute-start.1
  25.7 5.1 %collective-permute-start.2 = (bf16[32,34,1,16]{1,0,3,2:T(8,128)(2,1)S(1)}, bf16[32,34,1,16]{1,0,3,2:T(8,128)(2,1)S(1)}, u32[]{:S(2)}, u32[]{:S(2)}) collective-permute-start(bf16[32,34,1,16]{1,0,3,2:T(8,128)(2,1)S(1)} %get-tuple-element.42), channel_id=1, source_target_pairs={{0,16},{16,32},{32,48},{48,64},{64,80},{80,96},{96,112},{1,17},{17... | collective-permute-start | bytes 104456 | tf_op jit(solution)/shard_map/ppermute | solution.py:19
  28.9 5.7 %collective-permute-start.3 = (bf16[32,34,1,16]{1,0,3,2:T(8,128)(2,1)S(1)}, bf16[32,34,1,16]{1,0,3,2:T(8,128)(2,1)S(1)}, u32[]{:S(2)}, u32[]{:S(2)}) collective-permute-start(bf16[32,34,1,16]{1,0,3,2:T(8,128)(2,1)S(1)} %get-tuple-element.43), channel_id=1, source_target_pairs={{16,0},{32,16},{48,32},{64,48},{80,64},{96,80},{112,96},{17,1},{33... | collective-permute-start | bytes 104456 | tf_op jit(solution)/shard_map/ppermute | solution.py:22
  34.7 9.2 %collective-permute-start.4 = (bf16[32,34,10,1]{1,0,3,2:T(8,128)(2,1)S(1)}, bf16[32,34,10,1]{1,0,3,2:T(8,128)(2,1)S(1)}, u32[]{:S(2)}, u32[]{:S(2)}) collective-permute-start(bf16[32,34,10,1]{1,0,3,2:T(8,128)(2,1)S(1)} %get-tuple-element.40), channel_id=1, source_target_pairs={{0,1},{1,2},{2,3},{3,4},{4,5},{5,6},{6,7},{7,8},{8,9},{9,10},{10,1... | collective-permute-start | bytes 65288 | tf_op jit(solution)/shard_map/ppermute | solution.py:19
  41.7 5.8 %collective-permute-start.5 = (bf16[32,34,10,1]{1,0,3,2:T(8,128)(2,1)S(1)}, bf16[32,34,10,1]{1,0,3,2:T(8,128)(2,1)S(1)}, u32[]{:S(2)}, u32[]{:S(2)}) collective-permute-start(bf16[32,34,10,1]{1,0,3,2:T(8,128)(2,1)S(1)} %get-tuple-element.41), channel_id=1, source_target_pairs={{1,0},{2,1},{3,2},{4,3},{5,4},{6,5},{7,6},{8,7},{9,8},{10,9},{11,1... | collective-permute-start | bytes 65288 | tf_op jit(solution)/shard_map/ppermute | solution.py:22
  67.5 2.6 collective-permute-start.6
  68.8 4.4 collective-permute-start.7
  73.3 4.5 collective-permute-start.8
  76.5 4.7 collective-permute-start.9
  81.3 19.3 %collective-permute-start.10 = (bf16[64,18,6,1]{0,3,2,1:T(2,128)(2,1)S(1)}, bf16[64,18,6,1]{0,3,2,1:T(2,128)(2,1)S(1)}, u32[]{:S(2)}, u32[]{:S(2)}) collective-permute-start(bf16[64,18,6,1]{0,3,2,1:T(2,128)(2,1)S(1)} %get-tuple-element.54), channel_id=1, source_target_pairs={{0,1},{1,2},{2,3},{3,4},{4,5},{5,6},{6,7},{7,8},{8,9},{9,10},{10,1... | collective-permute-start | bytes 41480 | tf_op jit(solution)/shard_map/ppermute | solution.py:19
  86.0 14.6 %collective-permute-start.11 = (bf16[64,18,6,1]{0,3,2,1:T(2,128)(2,1)S(1)}, bf16[64,18,6,1]{0,3,2,1:T(2,128)(2,1)S(1)}, u32[]{:S(2)}, u32[]{:S(2)}) collective-permute-start(bf16[64,18,6,1]{0,3,2,1:T(2,128)(2,1)S(1)} %get-tuple-element.55), channel_id=1, source_target_pairs={{1,0},{2,1},{3,2},{4,3},{5,4},{6,5},{7,6},{8,7},{9,8},{10,9},{11,1... | collective-permute-start | bytes 41480 | tf_op jit(solution)/shard_map/ppermute | solution.py:22
  88.7 20.6 %all-to-all-start.2 = ((bf16[128,1,4,128]{0,2,1,3:T(4,128)(2,1)}), bf16[128,1,4,128]{0,2,1,3:T(4,128)(2,1)S(1)}, u32[]{:S(2)}, u32[]{:S(2)}) async-start(bf16[128,1,4,128]{0,2,1,3:T(4,128)(2,1)} %copy.141), calls=%async_computation.2 | async-start | bytes 262144 | tf_op jit(solution)/shard_map/all_to_all | solution.py:131
  109.9 17.9 %collective-permute-start.12 = (bf16[128,1,4,8]{0,3,2,1:T(8,128)(2,1)S(1)}, bf16[128,1,4,8]{0,3,2,1:T(8,128)(2,1)S(1)}, u32[]{:S(2)}, u32[]{:S(2)}) collective-permute-start(bf16[128,1,4,8]{0,3,2,1:T(8,128)(2,1)S(1)} %get-tuple-element.60), channel_id=1, source_target_pairs={{0,128},{1,129},{2,130},{3,131},{4,132},{5,133},{6,134},{7,135},{8... | collective-permute-start | bytes 24584 | tf_op jit(solution)/shard_map/ppermute | solution.py:19
  111.3 16.6 %collective-permute-start.13 = (bf16[128,1,4,8]{0,3,2,1:T(8,128)(2,1)S(1)}, bf16[128,1,4,8]{0,3,2,1:T(8,128)(2,1)S(1)}, u32[]{:S(2)}, u32[]{:S(2)}) collective-permute-start(bf16[128,1,4,8]{0,3,2,1:T(8,128)(2,1)S(1)} %get-tuple-element.61), channel_id=1, source_target_pairs={{128,0},{129,1},{130,2},{131,3},{132,4},{133,5},{134,6},{135,7},{1... | collective-permute-start | bytes 24584 | tf_op jit(solution)/shard_map/ppermute | solution.py:22
  127.9 16.6 %collective-permute-start.14 = (bf16[128,18,1,8]{0,3,2,1:T(8,128)(2,1)S(1)}, bf16[128,18,1,8]{0,3,2,1:T(8,128)(2,1)S(1)}, u32[]{:S(2)}, u32[]{:S(2)}) collective-permute-start(bf16[128,18,1,8]{0,3,2,1:T(8,128)(2,1)S(1)} %get-tuple-element.56), channel_id=1, source_target_pairs={{0,16},{16,32},{32,48},{48,64},{64,80},{80,96},{96,112},{1,17},{17... | collective-permute-start | bytes 110600 | tf_op jit(solution)/shard_map/ppermute | solution.py:19
  134.5 10.0 %collective-permute-start.15 = (bf16[128,18,1,8]{0,3,2,1:T(8,128)(2,1)S(1)}, bf16[128,18,1,8]{0,3,2,1:T(8,128)(2,1)S(1)}, u32[]{:S(2)}, u32[]{:S(2)}) collective-permute-start(bf16[128,18,1,8]{0,3,2,1:T(8,128)(2,1)S(1)} %get-tuple-element.57), channel_id=1, source_target_pairs={{16,0},{32,16},{48,32},{64,48},{80,64},{96,80},{112,96},{17,1},{33... | collective-permute-start | bytes 110600 | tf_op jit(solution)/shard_map/ppermute | solution.py:22
  140.5 85.9 %all-to-all-start.1 = ((bf16[8,2,128,1,4,8]{2,5,4,1,3,0:T(8,128)(2,1)}), bf16[8,2,128,1,4,8]{2,5,4,1,3,0:T(8,128)(2,1)}, u32[]{:S(2)}, u32[]{:S(2)}) async-start(bf16[8,2,128,1,4,8]{2,5,4,1,3,0:T(8,128)(2,1)} %copy.139), calls=%async_computation.1 | async-start | bytes 262144 | tf_op jit(solution)/shard_map/all_to_all | solution.py:43
  144.5 347.6 %all-reduce.2.cloned.1.call-start = ((), (), s32[]{:S(2)}) async-start(), calls=%async_computation.3 | async-start | bytes 2220032 | tf_op jit(solution)/shard_map/psum | solution.py:56
  144.6 5.8 %collective-permute-start.16 = (bf16[128,18,6,1]{0,3,2,1:T(2,128)(2,1)S(1)}, bf16[128,18,6,1]{0,3,2,1:T(2,128)(2,1)S(1)}, u32[]{:S(2)}, u32[]{:S(2)}) collective-permute-start(bf16[128,18,6,1]{0,3,2,1:T(2,128)(2,1)S(1)} %get-tuple-element.52), channel_id=1, source_target_pairs={{0,1},{1,2},{2,3},{3,4},{4,5},{5,6},{6,7},{7,8},{8,9},{9,10},{10,1... | collective-permute-start | bytes 82952 | tf_op jit(solution)/shard_map/ppermute | solution.py:19
  148.4 5.9 %collective-permute-start.17 = (bf16[128,18,6,1]{0,3,2,1:T(2,128)(2,1)S(1)}, bf16[128,18,6,1]{0,3,2,1:T(2,128)(2,1)S(1)}, u32[]{:S(2)}, u32[]{:S(2)}) collective-permute-start(bf16[128,18,6,1]{0,3,2,1:T(2,128)(2,1)S(1)} %get-tuple-element.53), channel_id=1, source_target_pairs={{1,0},{2,1},{3,2},{4,3},{5,4},{6,5},{7,6},{8,7},{9,8},{10,9},{11,1... | collective-permute-start | bytes 82952 | tf_op jit(solution)/shard_map/ppermute | solution.py:22
  159.0 25.0 %copy-start.2 = (bf16[64,32,8,16]{0,2,3,1:T(8,128)(2,1)}, bf16[64,32,8,16]{0,2,3,1:T(8,128)(2,1)S(1)}, u32[]{:S(2)}) copy-start(bf16[64,32,8,16]{0,2,3,1:T(8,128)(2,1)S(1)} %multiply_convert_fusion) | copy-start | bytes 1572868
  159.0 9.7 %collective-permute-start.18 = (bf16[64,1,8,16]{0,2,3,1:T(8,128)(2,1)S(1)}, bf16[64,1,8,16]{0,2,3,1:T(8,128)(2,1)S(1)}, u32[]{:S(2)}, u32[]{:S(2)}) collective-permute-start(bf16[64,1,8,16]{0,2,3,1:T(8,128)(2,1)S(1)} %get-tuple-element.48), channel_id=1, source_target_pairs={{0,128},{1,129},{2,130},{3,131},{4,132},{5,133},{6,134},{7,135},{8... | collective-permute-start | bytes 49160 | tf_op jit(solution)/shard_map/ppermute | solution.py:19
  163.3 5.5 %collective-permute-start.19 = (bf16[64,1,8,16]{0,2,3,1:T(8,128)(2,1)S(1)}, bf16[64,1,8,16]{0,2,3,1:T(8,128)(2,1)S(1)}, u32[]{:S(2)}, u32[]{:S(2)}) collective-permute-start(bf16[64,1,8,16]{0,2,3,1:T(8,128)(2,1)S(1)} %get-tuple-element.49), channel_id=1, source_target_pairs={{128,0},{129,1},{130,2},{131,3},{132,4},{133,5},{134,6},{135,7},{1... | collective-permute-start | bytes 49160 | tf_op jit(solution)/shard_map/ppermute | solution.py:22
  169.2 9.1 %collective-permute-start.20 = (bf16[64,34,1,16]{0,2,3,1:T(2,128)(2,1)S(1)}, bf16[64,34,1,16]{0,2,3,1:T(2,128)(2,1)S(1)}, u32[]{:S(2)}, u32[]{:S(2)}) collective-permute-start(bf16[64,34,1,16]{0,2,3,1:T(2,128)(2,1)S(1)} %get-tuple-element.46), channel_id=1, source_target_pairs={{0,16},{16,32},{32,48},{48,64},{64,80},{80,96},{96,112},{1,17},{17... | collective-permute-start | bytes 208904 | tf_op jit(solution)/shard_map/ppermute | solution.py:19
  173.5 10.5 %collective-permute-start.21 = (bf16[64,34,1,16]{0,2,3,1:T(2,128)(2,1)S(1)}, bf16[64,34,1,16]{0,2,3,1:T(2,128)(2,1)S(1)}, u32[]{:S(2)}, u32[]{:S(2)}) collective-permute-start(bf16[64,34,1,16]{0,2,3,1:T(2,128)(2,1)S(1)} %get-tuple-element.47), channel_id=1, source_target_pairs={{16,0},{32,16},{48,32},{64,48},{80,64},{96,80},{112,96},{17,1},{33... | collective-permute-start | bytes 208904 | tf_op jit(solution)/shard_map/ppermute | solution.py:22
  184.9 43.2 %collective-permute-start.22 = (bf16[64,34,10,1]{0,2,3,1:T(8,128)(2,1)}, bf16[64,34,10,1]{0,2,3,1:T(8,128)(2,1)}, u32[]{:S(2)}, u32[]{:S(2)}) collective-permute-start(bf16[64,34,10,1]{0,2,3,1:T(8,128)(2,1)} %get-tuple-element.44), channel_id=1, source_target_pairs={{0,1},{1,2},{2,3},{3,4},{4,5},{5,6},{6,7},{7,8},{8,9},{9,10},{10,1... | collective-permute-start | bytes 130568 | tf_op jit(solution)/shard_map/ppermute | solution.py:19
  189.8 38.3 %collective-permute-start.23 = (bf16[64,34,10,1]{0,2,3,1:T(8,128)(2,1)}, bf16[64,34,10,1]{0,2,3,1:T(8,128)(2,1)}, u32[]{:S(2)}, u32[]{:S(2)}) collective-permute-start(bf16[64,34,10,1]{0,2,3,1:T(8,128)(2,1)} %get-tuple-element.45), channel_id=1, source_target_pairs={{1,0},{2,1},{3,2},{4,3},{5,4},{6,5},{7,6},{8,7},{9,8},{10,9},{11,1... | collective-permute-start | bytes 130568 | tf_op jit(solution)/shard_map/ppermute | solution.py:22
  191.9 25.8 %copy-start.13 = (f32[3,3,3,64,128]{4,3,2,1,0:T(8,128)S(1)}, f32[3,3,3,64,128]{4,3,2,1,0:T(8,128)}, u32[]{:S(2)}) copy-start(f32[3,3,3,64,128]{4,3,2,1,0:T(8,128)} %fusion.30) | copy-start | bytes 2654212
  191.9 25.8 %copy-start.22 = (f32[128]{0:T(128)S(1)}, f32[128]{0:T(128)}, u32[]{:S(2)}) copy-start(f32[128]{0:T(128)} %get-tuple-element.36) | copy-start | bytes 1540
  191.9 25.8 %copy-start.24 = (f32[64]{0:T(128)S(1)}, f32[64]{0:T(128)}, u32[]{:S(2)}) copy-start(f32[64]{0:T(128)} %get-tuple-element.38) | copy-start | bytes 772
  (24 other events, 211.2 us)
Sparse Core Ops, SparseCore 0:
  226.5 265.5 all-reduce.1
where the time goes:
time: 512 us; the launch traced here: 506 us
  waiting for transfers between devices  277 us (54%)
  starting transfers between devices  82.7 us (16%)
  matrix products  53.1 us (10%)
  local copies, waits for them, and re-layouts  51.9 us (10%)
  other arithmetic  22 us (4%)
  between operations  15.1 us (3%)
    psum x1, waiting for transfers between devices, together(): total = lax.psum(jnp.concatenate([a.ravel() for a in arrays]), axis)  243 us
    ppermute x12, starting transfers between devices, padded_2(): lax.ppermute(lax.slice_in_dim(block, block.shape[dim] - width, None, axis...  48.4 us
    transpose x2, matrix products, weight_terms(): return jnp.transpose(result, (2, 3, 4, 0, 1))  28.6 us
    ppermute x12, waiting for transfers between devices, padded_2(): lax.ppermute(lax.slice_in_dim(block, 0, width, axis=dim), axis, backward)  25.1 us
    conv_general_dilated x4, matrix products, conv_valid(): lax.conv_general_dilated(padded[None], weight, (1, 1, 1), 'VALID', dimens...  24.5 us
    ppermute x12, starting transfers between devices, padded_2(): lax.ppermute(lax.slice_in_dim(block, 0, width, axis=dim), axis, backward)  18.5 us
    all_to_all x1, starting transfers between devices, on_device(): lax.all_to_all(cotangent, GZ, split_axis=3, concat_axis=1, tiled=True)  11.8 us
  transfers between devices with their start and end apart: 27, of which 11 were waited for; matrix products, arithmetic and copies ran while one was open for 18% of the time, Pallas kernels for 0%

commit v1 on v0

v1 whole, which is shorter than its diff:
```python
import math

import jax
import jax.numpy as jnp
from jax import lax
from jax.experimental import pallas as pl
from jax.experimental.pallas import tpu as pltpu
from jax.sharding import PartitionSpec as P

F32 = jnp.float32
BF16 = jnp.bfloat16
MESH = pl.DeviceIdType.MESH
GX, GY, GZ, GROUP = 2, 8, 16, 32
PITCH = 24
CHUNK_A, CHUNK_B = 16, 64


class Halo:
    def __init__(self, length, sides):
        self.length, self.sides = length, sides
        self.messages, self.staged, self.stage_rows, self.rows = [], {}, 0, 0
        for dx in (0, 1):
            for dy in (-1, 0, 1):
                for dz in (-1, 0, 1):
                    if not (dx or dy or dz):
                        continue
                    blocks, count = [], 0
                    for q, side in enumerate(sides):
                        if dy and dy not in side:
                            continue
                        if dx:
                            rows = 16 if dy else 32
                        elif dy:
                            rows = length if dz else 8 * length
                        else:
                            rows = 4 * length
                        blocks.append((q, count, rows))
                        count += rows
                    key = (dx, dy, 0 if dx else dz)
                    if key not in self.staged:
                        self.staged[key] = (self.stage_rows, blocks)
                        self.stage_rows += count
                    self.messages.append((dx, dy, dz, key, count, self.rows, blocks))
                    self.rows += count

    def grid(self, ref):
        return ref.reshape(self.length + 2, 6, PITCH, 128)

    def send(self, at, grids, stage, landed, send_sem, recv_sem):
        n = self.length
        gx, gy, gz = at
        edge = n - gx * (n - 1)
        for (dx, dy, dz), (start, blocks) in self.staged.items():
            ys = 4 if dy < 0 else 1
            zs = 15 if dz < 0 else 8
            for q, offset, rows in blocks:
                flat, grid = grids[q], self.grid(grids[q])
                row = start + offset
                if dx:
                    if dy:
                        tile = grid[edge, ys, 8:16, :]
                        value = jnp.concatenate([tile, tile], axis=0)
                    else:
                        value = grid[edge, 1:5, 8:16, :].reshape(32, 128)
                    stage[row : row + rows, :] = value.astype(BF16)
                elif dz == 0:
                    value = grid[1 : n + 1, ys, 8:16, :].reshape(8 * n, 128)
                    stage[row : row + rows, :] = value.astype(BF16)
                else:
                    for k, y in enumerate((ys,) if dy else (1, 2, 3, 4)):
                        value = flat[pl.ds((6 + y) * PITCH + zs, n, stride=6 * PITCH), :]
                        stage[row + k * n : row + (k + 1) * n, :] = value.astype(BF16)
        for dx, dy, dz, key, count, row, _ in self.messages:
            start = self.staged[key][0]
            target = (
                1 - gx if dx else gx,
                lax.rem(gy + (GY - dy), GY) if dy else gy,
                lax.rem(gz + (GZ - dz), GZ) if dz else gz,
            )
            pltpu.make_async_remote_copy(
                src_ref=stage.at[start : start + count],
                dst_ref=landed.at[row : row + count],
                send_sem=send_sem,
                recv_sem=recv_sem,
                device_id=target,
                device_id_type=MESH,
            ).start()

    def receive(self, at, grids, landed, recv_sem):
        n = self.length
        gx, gy, gz = at
        far = (n + 1) * (1 - gx)
        for grid in grids:
            self.grid(grid)[(n + 1) * gx, :, :, :] = jnp.zeros((6, PITCH, 128), F32)
        pltpu.make_async_copy(landed, landed, recv_sem).wait()
        inside_y = {-1: gy > 0, 0: None, 1: gy < GY - 1}
        inside_z = {-1: gz > 0, 0: None, 1: gz < GZ - 1}
        for dx, dy, dz, _, _, start, blocks in self.messages:
            yd = 0 if dy < 0 else 5
            zd = 7 if dz < 0 else 16
            tile = 8 * (dz + 1)
            keep = [c for c in (inside_y[dy], inside_z[dz]) if c is not None]
            for q, offset, rows in blocks:
                flat, grid = grids[q], self.grid(grids[q])
                row = start + offset

                def take(first, size):
                    value = landed[first : first + size, :].astype(F32)
                    for c in keep:
                        value = jnp.where(c, value, 0.0)
                    return value

                if dx and dy:
                    grid[far, yd, tile : tile + 8, :] = take(row, 16)[:8]
                elif dx:
                    grid[far, 1:5, tile : tile + 8, :] = take(row, 32).reshape(4, 8, 128)
                elif dz == 0:
                    grid[1 : n + 1, yd, 8:16, :] = take(row, 8 * n).reshape(n, 8, 128)
                else:
                    for k, y in enumerate((yd,) if dy else (1, 2, 3, 4)):
                        flat[pl.ds((6 + y) * PITCH + zd, n, stride=6 * PITCH), :] = take(row + k * n, n)


HALO_VOLUME = Halo(32, ((-1, 1),))
HALO_COARSE = Halo(16, ((-1, 1),))
HALO_GRAD_A = Halo(32, ((1,), (-1,)))


def row_block(jy, jz):
    ty, py = (0, jy - 1) if jy in (1, 2) else (1, 1 if jy == 0 else 0)
    tz, pz = (0, jz - 1) if jz in (1, 2) else (1, 1 if jz == 0 else 0)
    return (ty * 2 + tz) * 4 + py * 2 + pz


def fine_offset(shifted, parity):
    if not shifted:
        return 1 + parity
    return 0 if parity else 3


def lanes_at_least(shape, width, period=None):
    lane = lax.broadcasted_iota(jnp.int32, shape, len(shape) - 1)
    if period:
        lane = lax.rem(lane, period)
    return lane >= width


class Sum:
    def __init__(self, at, chunk, send, got, mids, out, sems):
        gx, gy, gz = at
        self.gx, self.gy, self.gz = at
        self.z, self.core = lax.div(gz, 2), lax.rem(gz, 2)
        self.rank = (gx * GY + gy) * 2 + self.core
        self.chunk, self.parts, self.got, self.mids, self.out, self.sems = chunk, send, got, mids, out, sems

    def plane_peer(self, rank):
        return (lax.div(rank, 16), lax.rem(lax.div(rank, 2), GY), self.z * 2 + lax.rem(rank, 2))

    def rows(self, k):
        return pl.ds(pl.multiple_of(k * self.chunk, self.chunk), self.chunk)

    def scatter(self):
        def issue(r, _):
            peer = lax.rem(self.rank + r, GROUP)
            pltpu.make_async_remote_copy(
                src_ref=self.parts.at[self.rows(peer)],
                dst_ref=self.got.at[self.rows(r - 1)],
                send_sem=self.sems.at[0],
                recv_sem=self.sems.at[1],
                device_id=self.plane_peer(peer),
                device_id_type=MESH,
            ).start()
            return 0

        lax.fori_loop(1, GROUP, issue, 0)

    def exchange(self):
        pltpu.make_async_copy(self.got, self.got, self.sems.at[1]).wait()

        def add(r, total):
            return total + self.got[self.rows(r), :].astype(F32)

        total = lax.fori_loop(0, GROUP - 1, add, self.parts[self.rows(self.rank), :].astype(F32))
        self.mids[self.rows(self.z), :] = total.astype(BF16)

        def issue(r, _):
            peer = lax.rem(self.z + r, 8)
            pltpu.make_async_remote_copy(
                src_ref=self.mids.at[self.rows(self.z)],
                dst_ref=self.mids.at[self.rows(self.z)],
                send_sem=self.sems.at[2],
                recv_sem=self.sems.at[3],
                device_id=(self.gx, self.gy, peer * 2 + self.core),
                device_id_type=MESH,
            ).start()
            return 0

        lax.fori_loop(1, 8, issue, 0)

    def gather(self):
        seven = self.mids.at[0 : 7 * self.chunk]
        pltpu.make_async_copy(seven, seven, self.sems.at[3]).wait()
        total = self.mids[0 : self.chunk, :].astype(F32)
        for k in range(1, 8):
            total = total + self.mids[k * self.chunk : (k + 1) * self.chunk, :].astype(F32)
        self.out[self.rows(self.rank), :] = total.astype(BF16)

        def issue(r, _):
            peer = lax.rem(self.rank + r, GROUP)
            pltpu.make_async_remote_copy(
                src_ref=self.out.at[self.rows(self.rank)],
                dst_ref=self.out.at[self.rows(self.rank)],
                send_sem=self.sems.at[4],
                recv_sem=self.sems.at[5],
                device_id=self.plane_peer(peer),
                device_id_type=MESH,
            ).start()
            return 0

        lax.fori_loop(1, GROUP, issue, 0)

    def finish(self):
        pltpu.make_async_copy(self.got, self.got, self.sems.at[5]).wait()

    def drain(self):
        seven = self.mids.at[0 : 7 * self.chunk]
        pltpu.make_async_copy(self.got, self.got, self.sems.at[0]).wait()
        pltpu.make_async_copy(seven, seven, self.sems.at[2]).wait()
        pltpu.make_async_copy(self.got, self.got, self.sems.at[4]).wait()


def kernel(
    scale_a, scale_b,
    volume, weight_a, bias_a, weight_b, bias_b, cot,
    features, grad_input, dwa, dba, dwb, dbb,
    fine, coarse, grad_c, fine_0, fine_1,
    lhs_a, lhs_b, lhs_c, lhs_f,
    pairs, mat_a, mat_b, mat_bt, mat_at,
    slope_a, feat, cot_here, gb, ga, dw,
    stage_v, land_v, stage_p, land_p, stage_g, land_g, stage_f, land_f,
    send_a, got_a, mid_a, out_a, send_b, got_b, mid_b, out_b,
    halo_sems, slab_sems, sems_a, sems_b,
):
    gx, gy, gz = lax.axis_index("gx"), lax.axis_index("gy"), lax.axis_index("gz")
    at = (gx, gy, gz)
    core = lax.rem(gz, 2)
    zero = jnp.zeros((32, 64), F32)

    barrier = pltpu.get_barrier_semaphore()

    def signal(target):
        pl.semaphore_signal(barrier, inc=1, device_id=target, device_id_type=MESH)

    def along_z(r, _):
        signal((gx, gy, lax.rem(gz + r, GZ)))
        return 0

    def in_plane(r, _):
        cell = lax.rem(gx * GY + gy + r, 16)
        for c in range(2):
            signal((lax.div(cell, GY), lax.rem(cell, GY), gz - core + c))
        return 0

    lax.fori_loop(1, GZ, along_z, 0)
    lax.fori_loop(1, 16, in_plane, 0)
    side = lax.rem(gz + GZ - 1 + 2 * core, GZ)
    for dx in (0, 1):
        for dy in (-1, 0, 1):
            if dx or dy:
                signal((1 - gx if dx else gx, lax.rem(gy + GY + dy, GY) if dy else gy, side))

    grid_v = HALO_VOLUME.grid(fine)

    def load_volume(x, _):
        rows = volume[pl.ds(pl.multiple_of(x * 32, 32), 32), :].astype(F32)
        grid_v[x + 1, 1:5, 8:16, :] = rows.reshape(4, 8, 128)
        return 0

    lax.fori_loop(0, 32, load_volume, 0)
    pl.semaphore_wait(barrier, 50)
    HALO_VOLUME.send(at, (fine,), stage_v, land_v, halo_sems.at[0], halo_sems.at[1])

    def slab_rows(k):
        return pl.ds(pl.multiple_of(k * 32, 32), 32)

    def send_cot(r, _):
        peer = lax.rem(gz + r, GZ)
        pltpu.make_async_remote_copy(
            src_ref=cot.at[slab_rows(peer)],
            dst_ref=cot_here.at[slab_rows(gz)],
            send_sem=slab_sems.at[0],
            recv_sem=slab_sems.at[1],
            device_id=(gx, gy, peer),
            device_id_type=MESH,
        ).start()
        return 0

    lax.fori_loop(1, GZ, send_cot, 0)
    cot_here[slab_rows(gz), :] = cot[slab_rows(gz), :]

    def make_pairs(k, _):
        w0 = weight_a[3 * k].astype(F32)
        w1 = weight_a[3 * k + 1].astype(F32)
        w2 = weight_a[3 * k + 2].astype(F32)
        for j, (left, right) in enumerate(((w0, zero), (w1, w0), (w2, w1), (zero, w2))):
            rows = pl.ds(pl.multiple_of(k * 128 + j * 32, 32), 32)
            pairs[rows, :] = jnp.concatenate([left, right], axis=1).astype(BF16)
        return 0

    lax.fori_loop(0, 9, make_pairs, 0)

    def pair(kxy, j):
        return pairs[pl.ds(pl.multiple_of(kxy * 128 + j * 32, 32), 32), :]

    def make_mats(kx, _):
        for t in range(4):
            ty, tz = t // 2, t % 2
            for py in range(2):
                jy = fine_offset(ty, py)
                for out_y in range(2):
                    ky = jy - out_y
                    inside = 0 <= ky <= 2
                    for pz in range(2):
                        jz = fine_offset(tz, pz)
                        row = kx * 512 + t * 128 + py * 64 + pz * 32
                        value = pair(kx * 3 + ky, jz) if inside else jnp.zeros((32, 128), BF16)
                        mat_a[pl.ds(pl.multiple_of(row, 32), 32), out_y * 128 : out_y * 128 + 128] = value
                    for out_z in range(2):
                        j = (3, 0)[out_z] if tz else (1, 2)[out_z]
                        row = kx * 128 + (out_y * 2 + out_z) * 32
                        value = (
                            pair((2 - kx) * 3 + 2 - ky, j) if inside else jnp.zeros((32, 128), BF16)
                        )
                        lane = (t * 2 + py) * 128
                        mat_at[pl.ds(pl.multiple_of(row, 32), 32), lane : lane + 128] = value
        parts = [(0, 0), (0, 2), (1, 0), (1, 2), (2, 0), (2, 2), (0, 1), (1, 1), (2, 1)]
        for j, (ky, kz) in enumerate(parts):
            row = kx * 640 + j * 64
            mat_b[pl.ds(pl.multiple_of(row, 64), 64), :] = weight_b[kx * 9 + ky * 3 + kz]
        mat_b[pl.ds(pl.multiple_of(kx * 640 + 576, 64), 64), :] = jnp.zeros((64, 128), BF16)
        for ky in range(3):
            for kz in range(3):
                lane = (ky * 3 + kz) * 128
                value = weight_b[(2 - kx) * 9 + (2 - ky) * 3 + 2 - kz]
                for c in range(2):
                    row = pl.ds(pl.multiple_of(kx * 128 + c * 64, 64), 64)
                    mat_bt[row, lane : lane + 128] = value
        return 0

    lax.fori_loop(0, 3, make_mats, 0)

    HALO_VOLUME.receive(at, (fine,), land_v, halo_sems.at[1])
    odd_z = lanes_at_least((6, 8, 128), 32, 64)
    odd_y = lanes_at_least((4, 8, 128), 64)
    upper = lanes_at_least((6, 8, 128), 64)

    def put(lhs, x, tile, value):
        rows = pl.ds(pl.multiple_of(x * 32, 32), 32)
        lhs[rows, tile * 128 : tile * 128 + 128] = value.reshape(32, 128).astype(BF16)

    def build_a(x, _):
        here = grid_v[x, :, 8:16, :]
        beside = jnp.where(odd_z, grid_v[x, :, 7:15, :], grid_v[x, :, 9:17, :])
        put(lhs_a, x, 0, here[1:5])
        put(lhs_a, x, 1, beside[1:5])
        put(lhs_a, x, 2, jnp.where(odd_y, here[0:4], here[2:6]))
        put(lhs_a, x, 3, jnp.where(odd_y, beside[0:4], beside[2:6]))
        return 0

    lax.fori_loop(0, 34, build_a, 0)
    grid_p = HALO_COARSE.grid(coarse)
    bias_a4 = jnp.concatenate([bias_a[...]] * 4, axis=1)

    def conv_a(i, _):
        row = i * 256
        value = bias_a4
        for kx in range(3):
            rows = pl.ds(pl.multiple_of(row + kx * 32, 32), 256)
            value = value + jnp.dot(
                lhs_a[rows, :], mat_a[kx * 512 : kx * 512 + 512, :], preferred_element_type=F32
            )
        sigma = jax.nn.sigmoid(value)
        active = value * sigma
        slope_a[pl.ds(pl.multiple_of(row, 256), 256), :] = sigma + active * (1.0 - sigma)
        total = active.reshape(4, 2, 32, 256)
        total = (total[:, 0] + total[:, 1]).reshape(128, 256)
        total = total[:, :128] + total[:, 128:]
        total = (total + pltpu.roll(total, 64, 1)) * 0.125
        total = total.astype(BF16).astype(F32)
        grid_p[pl.ds(1 + i * 4, 4), 1:5, 8:16, :] = total.reshape(4, 4, 8, 128)
        return 0

    lax.fori_loop(0, 4, conv_a, 0)
    HALO_COARSE.send(at, (coarse,), stage_p, land_p, halo_sems.at[2], halo_sems.at[3])

    send_b[1728:2048, :] = jnp.zeros((320, 128), BF16)
    send_a[464:512, :] = jnp.zeros((48, 128), BF16)
    HALO_COARSE.receive(at, (coarse,), land_p, halo_sems.at[3])

    def build_b(x, _):
        here = grid_p[x, :, 8:16, :]
        beside = jnp.where(upper, grid_p[x, :, 9:17, :], grid_p[x, :, 7:15, :])
        for ky in range(3):
            put(lhs_b, x, ky, beside[ky : ky + 4])
        put(lhs_b, x, 3, jnp.where(upper[:4], here[1:5], here[0:4]))
        put(lhs_b, x, 4, jnp.where(upper[:4], 0.0, here[2:6]))
        return 0

    lax.fori_loop(0, 18, build_b, 0)
    fifteen = cot_here.at[0:480]
    pltpu.make_async_copy(fifteen, fifteen, slab_sems.at[1]).wait()
    grid_g = HALO_COARSE.grid(grad_c)

    def conv_b(i, _):
        row = i * 256
        value = bias_b[...]
        for kx in range(3):
            rows = pl.ds(pl.multiple_of(row + kx * 32, 32), 256)
            value = value + jnp.dot(
                lhs_b[rows, :], mat_b[kx * 640 : kx * 640 + 640, :], preferred_element_type=F32
            )
        sigma = jax.nn.sigmoid(value)
        active = value * sigma
        rows = pl.ds(pl.multiple_of(row, 256), 256)
        feat[rows, :] = active.astype(BF16)
        grad = (cot_here[rows, :].astype(F32) * (sigma + active * (1.0 - sigma))).astype(BF16)
        gb[rows, :] = grad
        grid_g[pl.ds(1 + i * 8, 8), 1:5, 8:16, :] = grad.astype(F32).reshape(8, 4, 8, 128)
        return 0

    lax.fori_loop(0, 2, conv_b, 0)
    HALO_COARSE.send(at, (grad_c,), stage_g, land_g, halo_sems.at[4], halo_sems.at[5])

    def send_features(r, _):
        peer = lax.rem(gz + r, GZ)
        pltpu.make_async_remote_copy(
            src_ref=feat.at[slab_rows(peer)],
            dst_ref=features.at[slab_rows(gz)],
            send_sem=slab_sems.at[2],
            recv_sem=slab_sems.at[3],
            device_id=(gx, gy, peer),
            device_id_type=MESH,
        ).start()
        return 0

    lax.fori_loop(1, GZ, send_features, 0)
    features[slab_rows(gz), :] = feat[slab_rows(gz), :]

    across = (((0,), (0,)), ((), ()))
    along = (((1,), (1,)), ((), ()))

    def grad_of_b(kx, _):
        rows = pl.ds(pl.multiple_of(kx * 32, 32), 512)
        for t in range(5):
            value = lax.dot_general(
                lhs_b[rows, t * 128 : t * 128 + 128], gb[...], across, preferred_element_type=F32
            ).astype(BF16)
            places = (t * 3, t * 3 + 2) if t < 3 else ((1, 4) if t == 3 else (7,))
            for half, k in enumerate(places):
                row = pl.ds(pl.multiple_of((kx * 9 + k) * 64, 64), 64)
                send_b[row, :] = value[half * 64 : half * 64 + 64]
        return 0

    lax.fori_loop(0, 3, grad_of_b, 0)
    bias_sum = jnp.sum(gb[...].astype(F32), axis=0, keepdims=True)
    send_b[1728:1744, :] = jnp.broadcast_to(bias_sum, (16, 128)).astype(BF16)
    sum_b = Sum(at, CHUNK_B, send_b, got_b, mid_b, out_b, sems_b)
    sum_b.scatter()

    HALO_COARSE.receive(at, (grad_c,), land_g, halo_sems.at[5])

    def build_c(x, _):
        for kz in range(3):
            value = grid_g[x, :, 7 + kz : 15 + kz, :]
            for ky in range(3):
                put(lhs_c, x, ky * 3 + kz, value[ky : ky + 4])
        return 0

    lax.fori_loop(0, 18, build_c, 0)
    grids_f = [HALO_GRAD_A.grid(fine_0), HALO_GRAD_A.grid(fine_1)]

    def back_b(i, _):
        value = jnp.zeros((128, 128), F32)
        for kx in range(3):
            rows = pl.ds(pl.multiple_of(i * 128 + kx * 32, 32), 128)
            value = value + lax.dot_general(
                lhs_c[rows, :], mat_bt[kx * 128 : kx * 128 + 128, :], along, preferred_element_type=F32
            )
        value = value.astype(BF16).astype(F32) * 0.125
        value = jnp.broadcast_to(value.reshape(4, 1, 32, 128), (4, 2, 32, 128)).reshape(256, 128)
        rows = pl.ds(pl.multiple_of(i * 256, 256), 256)
        for py in range(2):
            lanes = slice(py * 128, py * 128 + 128)
            grad = (value * slope_a[rows, lanes]).astype(BF16)
            ga[rows, lanes] = grad
            grids_f[py][pl.ds(1 + i * 8, 8), 1:5, 8:16, :] = grad.astype(F32).reshape(8, 4, 8, 128)
        return 0

    lax.fori_loop(0, 4, back_b, 0)
    HALO_GRAD_A.send(at, (fine_0, fine_1), stage_f, land_f, halo_sems.at[6], halo_sems.at[7])

    def grad_of_a(kx, _):
        rows = pl.ds(pl.multiple_of(kx * 32, 32), 1024)
        for t in range(4):
            row = pl.ds(pl.multiple_of(kx * 512 + t * 128, 128), 128)
            dw[row, :] = lax.dot_general(
                lhs_a[rows, t * 128 : t * 128 + 128], ga[...], across, preferred_element_type=F32
            )
        return 0

    lax.fori_loop(0, 3, grad_of_a, 0)
    high = lanes_at_least((32, 128), 64)

    def block_sum(kx, ky, jz):
        total = None
        for out_y in range(2):
            row = kx * 512 + row_block(ky + out_y, jz) * 32
            part = dw[row : row + 32, out_y * 128 : out_y * 128 + 128]
            total = part if total is None else total + part
        return total

    for k in range(14):
        kx, ky, kz = k // 9, k // 3 % 3, k % 3
        value = block_sum(kx, ky, kz) + pltpu.roll(block_sum(kx, ky, kz + 1), 64, 1)
        other = jnp.zeros((32, 128), F32)
        if k + 14 < 27:
            kx, ky, kz = (k + 14) // 9, (k + 14) // 3 % 3, (k + 14) % 3
            other = pltpu.roll(block_sum(kx, ky, kz), 64, 1) + block_sum(kx, ky, kz + 1)
        send_a[k * 32 : k * 32 + 32, :] = jnp.where(high, other, value).astype(BF16)
    bias_sum = jnp.sum(ga[...].astype(F32), axis=0, keepdims=True)
    bias_sum = jnp.broadcast_to(bias_sum[:, :128] + bias_sum[:, 128:], (16, 128))
    send_a[448:464, :] = (bias_sum + pltpu.roll(bias_sum, 64, 1)).astype(BF16)
    sum_a = Sum(at, CHUNK_A, send_a, got_a, mid_a, out_a, sems_a)
    sum_a.scatter()
    sum_b.exchange()

    HALO_GRAD_A.receive(at, (fine_0, fine_1), land_f, halo_sems.at[7])

    def build_f(x, _):
        for q, grid in enumerate(grids_f):
            low = 1 - q
            here = grid[x, low : low + 5, 8:16, :]
            beside = jnp.where(
                upper[:5], grid[x, low : low + 5, 7:15, :], grid[x, low : low + 5, 9:17, :]
            )
            near, far = (slice(1, 5), slice(0, 4)) if q else (slice(0, 4), slice(1, 5))
            put(lhs_f, x, q, here[near])
            put(lhs_f, x, 2 + q, beside[near])
            put(lhs_f, x, 4 + q, here[far])
            put(lhs_f, x, 6 + q, beside[far])
        return 0

    lax.fori_loop(0, 34, build_f, 0)
    sum_a.exchange()

    def back_a(i, _):
        value = jnp.zeros((256, 128), F32)
        for kx in range(3):
            rows = pl.ds(pl.multiple_of(i * 256 + kx * 32, 32), 256)
            value = value + lax.dot_general(
                lhs_f[rows, :], mat_at[kx * 128 : kx * 128 + 128, :], along, preferred_element_type=F32
            )
        grad_input[pl.ds(pl.multiple_of(i * 256, 256), 256), :] = value.astype(BF16)
        return 0

    lax.fori_loop(0, 4, back_a, 0)
    sum_b.gather()
    sum_a.gather()

    fifteen_out = features.at[0:480]
    pltpu.make_async_copy(fifteen_out, fifteen_out, slab_sems.at[3]).wait()
    sum_b.finish()
    dwb[...] = out_b[0:1728, :].astype(F32) * scale_b
    dbb[...] = out_b[1728:1744, :].astype(F32)[0:1] * scale_b
    sum_a.finish()
    for k in range(27):
        row = k % 14 * 32
        value = out_a[row : row + 32, :].astype(F32) * scale_a
        if k >= 14:
            value = pltpu.roll(value, 64, 1)
        dwa[k * 32 : k * 32 + 32, :] = value[:, :64]
    dba[...] = out_a[448:464, :].astype(F32)[0:1, :64] * scale_a

    for sem, ref in ((0, land_v), (2, land_p), (4, land_g), (6, land_f)):
        pltpu.make_async_copy(ref, ref, halo_sems.at[sem]).wait()
    pltpu.make_async_copy(fifteen, fifteen, slab_sems.at[0]).wait()
    pltpu.make_async_copy(fifteen, fifteen, slab_sems.at[2]).wait()
    sum_b.drain()
    sum_a.drain()


def on_device(volume, weight_a, bias_a, weight_b, bias_b, cotangent):
    cells = 64 * 64 * 256
    scale_a, scale_b = 1.0 / math.sqrt(cells), 1.0 / math.sqrt(cells // 8)
    rows = volume.reshape(32, 32, 4, 2, 8, 2).transpose(1, 2, 4, 3, 5, 0).reshape(1024, 128)
    cot = cotangent.reshape(128, 4, 16, 8).transpose(2, 1, 3, 0).reshape(512, 128)

    def vm(shape, dtype):
        return pltpu.VMEM(shape, dtype)

    hv, hc, hf = HALO_VOLUME, HALO_COARSE, HALO_GRAD_A
    fine_rows, coarse_rows = 34 * 6 * PITCH, 18 * 6 * PITCH
    scratch = [
        vm((fine_rows, 128), F32), vm((coarse_rows, 128), F32), vm((coarse_rows, 128), F32),
        vm((fine_rows, 128), F32), vm((fine_rows, 128), F32),
        vm((1088, 512), BF16), vm((576, 640), BF16), vm((576, 1152), BF16), vm((1088, 1024), BF16),
        vm((1152, 128), BF16), vm((1536, 256), BF16), vm((1920, 128), BF16), vm((384, 1152), BF16),
        vm((384, 1024), BF16),
        vm((1024, 256), F32), vm((512, 128), BF16), vm((512, 128), BF16), vm((512, 128), BF16),
        vm((1024, 256), BF16), vm((1536, 256), F32),
        vm((hv.stage_rows, 128), BF16), vm((hv.rows, 128), BF16),
        vm((hc.stage_rows, 128), BF16), vm((hc.rows, 128), BF16),
        vm((hc.stage_rows, 128), BF16), vm((hc.rows, 128), BF16),
        vm((hf.stage_rows, 128), BF16), vm((hf.rows, 128), BF16),
    ]
    for chunk in (CHUNK_A, CHUNK_B):
        for count in (GROUP, GROUP - 1, 8, GROUP):
            scratch.append(vm((count * chunk, 128), BF16))
    scratch += [pltpu.SemaphoreType.DMA((k,)) for k in (8, 4, 6, 6)]
    outs = [
        jax.ShapeDtypeStruct((512, 128), BF16),
        jax.ShapeDtypeStruct((1024, 128), BF16),
        jax.ShapeDtypeStruct((864, 64), F32),
        jax.ShapeDtypeStruct((1, 64), F32),
        jax.ShapeDtypeStruct((1728, 128), F32),
        jax.ShapeDtypeStruct((1, 128), F32),
    ]
    space = pl.BlockSpec(memory_space=pltpu.VMEM)
    features, grad_input, dwa, dba, dwb, dbb = pl.pallas_call(
        lambda *refs: kernel(scale_a, scale_b, *refs),
        name="window",
        out_shape=outs,
        in_specs=[space] * 6,
        out_specs=[space] * 6,
        scratch_shapes=scratch,
        compiler_params=pltpu.CompilerParams(collective_id=0, has_side_effects=True),
    )(
        rows,
        weight_a.reshape(27, 32, 64),
        bias_a.reshape(1, 64),
        weight_b.reshape(27, 64, 128),
        bias_b.reshape(1, 128),
        cot,
    )
    features = features.reshape(16, 4, 8, 128).transpose(3, 1, 0, 2).reshape(128, 1, 4, 128)
    grad_input = grad_input.reshape(32, 4, 8, 2, 2, 32).transpose(5, 0, 1, 3, 2, 4).reshape(32, 32, 8, 16)
    return (
        features,
        grad_input,
        dwa.reshape(3, 3, 3, 32, 64),
        dba.reshape(64),
        dwb.reshape(3, 3, 3, 64, 128),
        dbb.reshape(128),
    )


def solution(mesh):
    return jax.shard_map(
        on_device,
        mesh=mesh,
        in_specs=(P(None, "gx", "gy", "gz"), P(), P(), P(), P(), P(None, ("gx", "gz"), "gy", None)),
        out_specs=(P(None, ("gx", "gz"), "gy", None), P(None, "gx", "gy", "gz"), P(), P(), P(), P()),
        check_vma=False,
    )
```

time: 512 us -> 73.7 us (0.14); the launches traced: 506 us -> 73.5 us
  waiting for transfers between devices: 277 us -> 0 us
  starting transfers between devices: 82.7 us -> 0 us
  Pallas kernels: 0 us -> 58.2 us
  matrix products: 53.1 us -> 0 us
  local copies, waits for them, and re-layouts: 51.9 us -> 14.6 us
  other arithmetic: 22 us -> 0 us
  between operations: 15.1 us -> 0.69 us
    psum x1 -> x0, waiting for transfers between devices: 243 us -> none  [together(): total = lax.psum(jnp.concatenate([a.ravel() for a in arrays]), axis)]
    ppermute x24 -> x0, starting transfers between devices: 66.9 us -> none  [the longest x12 48.4 us: padded_2(): lax.ppermute(lax.slice_in_dim(block, block.shape[dim] - width, None, axis...]
    pallas_call x0 -> x1, Pallas kernels: none -> 58.2 us  [on_device(): pl.pallas_call(lambda *refs: kernel(scale_a, scale_b, *refs), name='windo...]
    transpose x2 -> x0, matrix products: 28.6 us -> none  [weight_terms(): return jnp.transpose(result, (2, 3, 4, 0, 1))]
    ppermute x24 -> x0, waiting for transfers between devices: 28.1 us -> none  [the longest x12 25.1 us: padded_2(): lax.ppermute(lax.slice_in_dim(block, 0, width, axis=dim), axis, backward)]
    conv_general_dilated x4 -> x0, matrix products: 24.5 us -> none  [conv_valid(): lax.conv_general_dilated(padded[None], weight, (1, 1, 1), 'VALID', dimens...]
    all_to_all x2 -> x0, starting transfers between devices: 15.8 us -> none  [the longest x1 11.8 us: on_device(): lax.all_to_all(cotangent, GZ, split_axis=3, concat_axis=1, tiled=True)]
    broadcast_in_dim x4 -> x0, local copies, waits for them, and re-layouts: 10.9 us -> none  [the longest x3 10.2 us: conv_valid(): padded[None]]
  transfers between devices with their start and end apart: 27 -> 0, of which waited for: 11 -> 0; matrix products, arithmetic and copies ran while one was open for 18% -> 0% of each run, Pallas kernels for 0% -> 0%
where the time goes in v1:
time: 73.7 us; the launch traced here: 73.5 us
  Pallas kernels  58.2 us (79%)
  local copies, waits for them, and re-layouts  14.6 us (20%)
    pallas_call x1, Pallas kernels, on_device(): pl.pallas_call(lambda *refs: kernel(scale_a, scale_b, *refs), name='windo...  58.2 us
    reshape x2, local copies, waits for them, and re-layouts, on_device(): volume.reshape(32, 32, 4, 2, 8, 2).transpose(1, 2, 4, 3, 5, 0)  5.05 us
    unnamed x16, local copies, waits for them, and re-layouts  4.58 us
    transpose x1, local copies, waits for them, and re-layouts, on_device(): grad_input.reshape(32, 4, 8, 2, 2, 32).transpose(5, 0, 1, 3, 2, 4)  2.91 us

profile of v1, /device:TPU:1, one launch (start us, length us, event | category | flops | bytes accessed | tf_op | source)
XLA Modules:
  0.0 73.5 jit_solution(6238526176413733695)
XLA Ops:
  0.6 1.0 %copy.17 = bf16[128,1,4,128]{0,3,2,1:T(8,128)(2,1)S(1)} copy(bf16[128,1,4,128]{3,2,1,0:T(4,128)(2,1)} %param.11) | data formatting | bytes 262144 | tf_op args[5]
  1.7 0.7 copy.18
  2.4 3.8 %copy.16 = bf16[32,32,4,2,8,2]{0,5,3,4,2,1:T(2,128)(2,1)S(1)} copy(bf16[32,32,4,2,8,2]{1,5,4,3,2,0:T(2,128)(2,1)} %bitcast.24) | data formatting | bytes 524288 | tf_op jit(solution)/shard_map/reshape | solution.py:595
  6.2 1.2 %reshape.61.refs_0_ = bf16[1024,128]{1,0:T(8,128)(2,1)} reshape(bf16[32,4,8,2,2,32]{5,4,3,2,1,0:T(2,128)(2,1)S(1)} %bitcast.23) | data formatting | bytes 524288 | tf_op jit(solution)/shard_map/reshape | solution.py:595
  7.4 58.2 %window.1 = (bf16[512,128]{1,0:T(8,128)(2,1)}, bf16[1024,128]{1,0:T(8,128)(2,1)}, f32[864,64]{1,0:T(8,128)}, f32[1,64]{1,0:T(1,128)}, f32[1728,128]{1,0:T(8,128)}, /*index=5*/f32[1,128]{1,0:T(1,128)}) custom-call(bf16[1024,128]{1,0:T(8,128)(2,1)} %reshape.61.refs_0_, bf16[27,32,64]{2,1,0:T(8,128)(2,1)} %bitcast.32, f32[1,64]{1,0:T(1,128)} %bitcast.34, ...), custom_call_target="tpu_custom_call" | custom-call | tf_op jit(solution)/shard_map/window/pallas_call | solution.py:629
  65.6 0.0 copy-start.2
  65.6 1.0 %copy.23 = bf16[16,4,8,128]{3,2,0,1:T(8,128)(2,1)S(1)} copy(bf16[16,4,8,128]{3,2,1,0:T(8,128)(2,1)} %bitcast.33) | data formatting | bytes 262144 | tf_op jit(solution)/shard_map/reshape | solution.py:645
  66.6 0.8 %copy.21 = bf16[128,1,4,128]{3,2,1,0:T(4,128)(2,1)} copy(bf16[128,1,4,128]{0,3,2,1:T(8,128)(2,1)S(1)} %bitcast.28) | data formatting | bytes 262144
  67.4 0.0 copy-done.2
  67.4 0.4 reshape.70
  67.8 0.0 copy-start.1
  67.8 2.9 %copy.20 = bf16[32,32,4,2,8,2]{1,5,4,3,2,0:T(2,128)(2,1)} copy(bf16[32,32,4,2,8,2]{0,5,3,4,2,1:T(2,128)(2,1)S(1)} %bitcast.22) | data formatting | bytes 524288 | tf_op jit(solution)/shard_map/transpose | solution.py:646
  70.7 0.0 copy-start
  70.7 0.0 copy-done.1
  70.7 0.0 copy-start.4
  70.7 0.8 %copy.28 = f32[3,3,3,32,64]{4,3,2,1,0:T(8,128)} copy(f32[3,3,3,32,64]{4,3,2,1,0:T(8,128)S(1)} %bitcast.31) | data formatting | bytes 442368
  71.5 0.0 copy-done.4
  71.5 0.5 copy.29
  72.0 0.0 copy-done
  72.1 0.0 copy-start.3
  72.1 0.9 %copy.30 = f32[3,3,3,64,128]{4,3,2,1,0:T(8,128)} copy(f32[3,3,3,64,128]{4,3,2,1,0:T(8,128)S(1)} %bitcast.26) | data formatting | bytes 1769472
  73.0 0.0 copy-done.3
  73.0 0.5 copy.31
Async XLA Ops:
  65.6 1.8 %copy-start.2 = (bf16[1024,128]{1,0:T(8,128)(2,1)S(1)}, bf16[1024,128]{1,0:T(8,128)(2,1)}, u32[]{:S(2)}) copy-start(bf16[1024,128]{1,0:T(8,128)(2,1)} %get-tuple-element.13) | copy-start | bytes 786436
  67.8 2.9 %copy-start.1 = (f32[864,64]{1,0:T(8,128)S(1)}, f32[864,64]{1,0:T(8,128)}, u32[]{:S(2)}) copy-start(f32[864,64]{1,0:T(8,128)} %get-tuple-element.14) | copy-start | bytes 663556
  70.7 1.3 %copy-start = (f32[1728,128]{1,0:T(8,128)S(1)}, f32[1728,128]{1,0:T(8,128)}, u32[]{:S(2)}) copy-start(f32[1728,128]{1,0:T(8,128)} %get-tuple-element.16) | copy-start | bytes 2654212
  70.7 0.8 %copy-start.4 = (f32[1,64]{1,0:T(1,128)S(1)}, f32[1,64]{1,0:T(1,128)}, u32[]{:S(2)}) copy-start(f32[1,64]{1,0:T(1,128)} %get-tuple-element.15) | copy-start | bytes 772
  72.1 0.9 %copy-start.3 = (f32[1,128]{1,0:T(1,128)S(1)}, f32[1,128]{1,0:T(1,128)}, u32[]{:S(2)}) copy-start(f32[1,128]{1,0:T(1,128)} %get-tuple-element.17) | copy-start | bytes 1540
